TPU v7x, 32 devices: a whole 2x2x4 slice. The times are simulated.
32 devices in a mesh: pr: 8 (over y, x, core), pc: 4 (over z).
Axes of the slice: x: 2, y: 2, z: 4, core: 2. Of those that a mesh axis runs over, the one named last changes fastest.
Arguments:
- pair_array: bfloat16 [256, 256, 128], P('pr', 'pc'), may hold values from -6 to 6
- left_weight: bfloat16 [128, 128], replicated, may hold values from -0.5 to 0.5
- right_weight: bfloat16 [128, 128], replicated, may hold values from -0.5 to 0.5
- left_gate: bfloat16 [128, 128], replicated, may hold values from -0.5 to 0.5
- right_gate: bfloat16 [128, 128], replicated, may hold values from -0.5 to 0.5
- mid_gain: float32 [128], replicated, may hold values from 0.25 to 1.75
- out_weight: bfloat16 [128, 128], replicated, may hold values from -0.5 to 0.5
- out_gate: bfloat16 [128, 128], replicated, may hold values from -0.5 to 0.5
Outputs:
- pair_update: bfloat16 [256, 256, 128], P('pr', 'pc')
All inputs are finite; a program needn't handle non-finite values.
Results may differ from a plain program's by a relative error of at most 0.012.
Values may be sent and summed in bfloat16 or wider, within the bound.
A program may use at most 128 MiB of HBM per device.

v0:
```python
import jax
import jax.numpy as jnp
from jax import lax
from jax.sharding import PartitionSpec as P


def unit_channels(values, channel_gain):
    centred = values - jnp.mean(values, axis=-1, keepdims=True)
    return (
        centred
        * lax.rsqrt(jnp.mean(centred * centred, axis=-1, keepdims=True) + 1e-05)
        * channel_gain
    )


def make_factors(pair_in, left_weight, right_weight, left_gate, right_gate):
    left = jnp.einsum("ijc,cd->ijd", pair_in, left_weight, preferred_element_type=jnp.float32)
    left = left * jax.nn.sigmoid(
        jnp.einsum("ijc,cd->ijd", pair_in, left_gate, preferred_element_type=jnp.float32)
    )
    right = jnp.einsum("ijc,cd->ijd", pair_in, right_weight, preferred_element_type=jnp.float32)
    right = right * jax.nn.sigmoid(
        jnp.einsum("ijc,cd->ijd", pair_in, right_gate, preferred_element_type=jnp.float32)
    )
    return (pair_in, left.astype(jnp.bfloat16), right.astype(jnp.bfloat16))


def to_pair(mixed, ready, mid_gain, out_weight, out_gate):
    scaled = unit_channels(mixed.astype(jnp.float32), mid_gain).astype(jnp.bfloat16)
    scaled = lax.optimization_barrier(scaled)
    gate = jax.nn.sigmoid(
        jnp.einsum("ijc,cd->ijd", ready, out_gate, preferred_element_type=jnp.float32)
    )
    return (
        jnp.einsum("ijd,dc->ijc", scaled, out_weight, preferred_element_type=jnp.float32) * gate
    ).astype(jnp.bfloat16)


def on_device(
    pair_array, left_weight, right_weight, left_gate, right_gate, mid_gain, out_weight, out_gate
):
    ready, left, right = make_factors(pair_array, left_weight, right_weight, left_gate, right_gate)
    count = pair_array.shape[0] * lax.axis_size("pr")
    left_lines, right_lines = (
        lax.all_to_all(left, "pr", split_axis=2, concat_axis=0, tiled=True),
        lax.all_to_all(right, "pr", split_axis=2, concat_axis=0, tiled=True),
    )
    strip = jnp.einsum(
        "kid,kjd->ijd",
        lax.all_gather(left_lines, "pc", axis=1, tiled=True),
        right_lines,
        preferred_element_type=jnp.float32,
    )
    strip = (strip * count ** (-0.5)).astype(jnp.bfloat16)
    mixed = lax.all_to_all(strip, "pr", split_axis=0, concat_axis=2, tiled=True)
    return to_pair(mixed, ready, mid_gain, out_weight, out_gate)


def solution(mesh):
    return jax.shard_map(
        on_device,
        mesh=mesh,
        in_specs=(P("pr", "pc", None), P(), P(), P(), P(), P(), P(), P()),
        out_specs=P("pr", "pc", None),
        check_vma=False,
    )
```

profile of v0, /device:TPU:0, one launch (start us, length us, event | category | flops | bytes accessed | tf_op | source)
XLA Modules:
  0.0 104.0 jit_solution(1541400130074911763)
XLA Ops:
  6.5 0.0 copy-start
  6.5 0.0 all-gather.2.cloned.1.call-start
  6.5 1.0 copy-done
  7.6 1.0 fusion.24
  8.6 1.2 %fusion.14 = bf16[32,64,128]{2,1,0:T(8,128)(2,1)S(1)} fusion(f32[32,64,128]{2,1,0:T(8,128)S(1)} %fusion.24, bf16[32,64,128]{2,1,0:T(8,128)(2,1)S(1)} %copy-done, bf16[128,128]{1,0:T(8,128)(2,1)} %param.11), kind=kOutput, calls=%fused_computation.22 | convolution fusion | flops 68419584 | bytes 2129920 | tf_op jit(solution)/shard_map/ijc,cd->ijd/dot_general | solution.py:19
  9.8 1.6 %copy.25 = bf16[32,64,128]{1,0,2:T(8,128)(2,1)S(1)} copy(bf16[32,64,128]{2,1,0:T(8,128)(2,1)S(1)} %fusion.14) | data formatting | bytes 1048576 | tf_op jit(solution)/shard_map/convert_element_type | solution.py:25
  11.4 0.7 reshape.28
  12.2 14.7 %all_to_all.45 = bf16[8,2,16384]{2,1,0:T(2,128)(2,1)S(1)} all-to-all(bf16[8,2,16384]{2,1,0:T(2,128)(2,1)S(1)} %reshape.28), channel_id=1, replica_groups=mesh['pr'=8,'pc'=4] {'pr'}, dimensions={0} | all-to-all | bytes 1048576 | tf_op jit(solution)/shard_map/all_to_all | solution.py:45
  26.8 0.7 reshape.29
  27.5 0.0 copy-start.1
  27.5 0.4 copy.27
  27.9 0.0 copy-start.4
  28.0 1.6 %copy.28 = bf16[256,64,16]{0,1,2:T(8,128)(2,1)} copy(bf16[256,64,16]{1,2,0:T(8,128)(2,1)S(1)} %bitcast.66) | data formatting | bytes 1048576 | tf_op jit(solution)/shard_map/all_to_all | solution.py:45
  29.6 0.0 all-gather.2.cloned.1.call-update
  29.6 0.0 copy-done.1
  29.6 0.3 fusion.27
  29.9 0.0 copy-done.4
  29.9 0.4 fusion.15
  30.4 1.6 %copy.22 = bf16[32,64,128]{1,0,2:T(8,128)(2,1)S(1)} copy(bf16[32,64,128]{2,1,0:T(8,128)(2,1)S(1)} %fusion.15) | data formatting | bytes 1048576 | tf_op jit(solution)/shard_map/convert_element_type | solution.py:25
  32.0 0.7 reshape.30
  32.7 12.1 %all_to_all.46 = bf16[8,2,16384]{2,1,0:T(2,128)(2,1)S(1)} all-to-all(bf16[8,2,16384]{2,1,0:T(2,128)(2,1)S(1)} %reshape.30), channel_id=1, replica_groups=mesh['pr'=8,'pc'=4] {'pr'}, dimensions={0} | all-to-all | bytes 1048576 | tf_op jit(solution)/shard_map/all_to_all | solution.py:46
  44.8 0.7 reshape.31
  45.5 0.4 copy.24
  45.9 28.9 %all-gather.2.cloned.1.call-done = bf16[256,256,16]{0,1,2:T(8,128)(2,1)} async-done(((bf16[256,64,16]{0,1,2:T(8,128)(2,1)}), bf16[256,256,16]{0,1,2:T(8,128)(2,1)}) %all-gather.2.cloned.1.call-update) | async-done | bytes 2097168 | tf_op jit(solution)/shard_map/all_gather | solution.py:50
  74.8 2.4 %fusion.18 = bf16[256,64,16]{0,1,2:T(8,128)(2,1)S(1)} fusion(bf16[256,256,16]{0,1,2:T(8,128)(2,1)} %all-gather.2.cloned.1.call-done, bf16[256,64,16]{1,2,0:T(8,128)(2,1)S(1)} %bitcast.61), kind=kOutput, calls=%fused_computation.26 | convolution fusion | flops 134742016 | bytes 3145728 | tf_op jit(solution)/shard_map/kid,kjd->ijd/dot_general | solution.py:48
  77.2 0.0 copy-start.5
  77.2 1.0 copy.30
  78.1 1.5 %reshape.32 = bf16[8,2,16384]{2,1,0:T(2,128)(2,1)} reshape(bf16[256,16,64]{2,1,0:T(8,128)(2,1)S(1)} %bitcast.64) | data formatting | bytes 1048576
  79.6 3.7 %all-to-all-start.2 = ((bf16[8,2,16384]{2,1,0:T(2,128)(2,1)}), bf16[8,2,16384]{2,1,0:T(2,128)(2,1)S(1)}, u32[]{:S(2)}, u32[]{:S(2)}) async-start(bf16[8,2,16384]{2,1,0:T(2,128)(2,1)} %reshape.32), calls=%async_computation.2 | async-start | bytes 1048576 | tf_op jit(solution)/shard_map/all_to_all | solution.py:55
  83.3 0.0 copy-done.5
  83.3 0.4 fusion.13
  83.8 9.3 %all-to-all-done.2 = bf16[8,2,16384]{2,1,0:T(2,128)(2,1)S(1)} async-done(((bf16[8,2,16384]{2,1,0:T(2,128)(2,1)}), bf16[8,2,16384]{2,1,0:T(2,128)(2,1)S(1)}, u32[]{:S(2)}, u32[]{:S(2)}) %all-to-all-start.2) | async-done | bytes 524320 | tf_op jit(solution)/shard_map/all_to_all | solution.py:55
  93.0 0.7 reshape.33
  93.7 0.2 convert_bitcast_fusion
  93.9 0.2 fusion.19
  94.1 0.4 multiply_reduce_fusion
  94.5 0.0 copy-start.3
  94.5 0.3 copy.31
  94.8 0.4 copy-done.3
  95.2 0.0 copy-start.2
  95.2 0.5 fusion.2
  95.6 0.3 copy-done.2
  95.9 1.3 %fusion.17 = bf16[32,64,128]{2,1,0:T(8,128)(2,1)} fusion(f32[32,64,128]{2,1,0:T(8,128)S(1)} %fusion.13, bf16[32,64,128]{1,2,0:T(8,128)(2,1)S(1)} %fusion.2, bf16[128,128]{1,0:T(8,128)(2,1)S(1)} %copy-done.2), kind=kOutput, calls=%fused_computation.25 | convolution fusion | flops 67633152 | bytes 2129920 | tf_op jit(solution)/shard_map/ijd,dc->ijc/dot_general | solution.py:35
  (2 shorter events, 0.0 us)
Async XLA Ops:
  6.5 1.0 %copy-start = (bf16[32,64,128]{2,1,0:T(8,128)(2,1)S(1)}, bf16[32,64,128]{2,1,0:T(8,128)(2,1)}, u32[]{:S(2)}) copy-start(bf16[32,64,128]{2,1,0:T(8,128)(2,1)} %param.8) | copy-start | bytes 1572868
  6.5 68.3 %all-gather.2.cloned.1.call-start = ((), (), s32[]{:S(2)}) async-start(), calls=%async_computation.3 | async-start | bytes 2621440 | tf_op jit(solution)/shard_map/all_gather | solution.py:50
  27.5 2.1 %copy-start.1 = (bf16[128,128]{1,0:T(8,128)(2,1)S(1)}, bf16[128,128]{1,0:T(8,128)(2,1)}, u32[]{:S(2)}) copy-start(bf16[128,128]{1,0:T(8,128)(2,1)} %param.10) | copy-start | bytes 98308
  27.9 2.0 %copy-start.4 = (bf16[128,128]{1,0:T(8,128)(2,1)S(1)}, bf16[128,128]{1,0:T(8,128)(2,1)}, u32[]{:S(2)}) copy-start(bf16[128,128]{1,0:T(8,128)(2,1)} %param.12) | copy-start | bytes 98308
  77.2 6.2 %copy-start.5 = (bf16[128,128]{1,0:T(8,128)(2,1)S(1)}, bf16[128,128]{1,0:T(8,128)(2,1)}, u32[]{:S(2)}) copy-start(bf16[128,128]{1,0:T(8,128)(2,1)} %param.15) | copy-start | bytes 98308
  79.6 13.4 %all-to-all-start.2 = ((bf16[8,2,16384]{2,1,0:T(2,128)(2,1)}), bf16[8,2,16384]{2,1,0:T(2,128)(2,1)S(1)}, u32[]{:S(2)}, u32[]{:S(2)}) async-start(bf16[8,2,16384]{2,1,0:T(2,128)(2,1)} %reshape.32), calls=%async_computation.2 | async-start | bytes 1048576 | tf_op jit(solution)/shard_map/all_to_all | solution.py:55
  94.5 0.7 copy-start.3
  95.2 0.8 copy-start.2
Sparse Core Ops, SparseCore 0:
  29.7 45.0 all-gather.1
where the time goes:
time: 105 us; the launch traced here: 104 us
  waiting for transfers between devices  38.2 us (36%)
  blocking collectives  26.8 us (26%)
  between operations  13.6 us (13%)
  local copies, waits for them, and re-layouts  13.5 us (13%)
  matrix products  6.96 us (7%)
  starting transfers between devices  3.68 us (4%)
  other arithmetic  1.27 us (1%)
    all_gather x1, waiting for transfers between devices, on_device(): lax.all_gather(left_lines, 'pc', axis=1, tiled=True)  28.9 us
    all_to_all x1, blocking collectives, on_device(): lax.all_to_all(left, 'pr', split_axis=2, concat_axis=0, tiled=True)  14.7 us
    all_to_all x1, blocking collectives, on_device(): lax.all_to_all(right, 'pr', split_axis=2, concat_axis=0, tiled=True)  12.1 us
    all_to_all x1, waiting for transfers between devices, on_device(): mixed = lax.all_to_all(strip, 'pr', split_axis=0, concat_axis=2, tiled=True)  9.25 us
    unnamed x18, local copies, waits for them, and re-layouts  6.59 us
    all_to_all x1, starting transfers between devices, on_device(): mixed = lax.all_to_all(strip, 'pr', split_axis=0, concat_axis=2, tiled=True)  3.67 us
    convert_element_type x2, local copies, waits for them, and re-layouts, make_factors(): return (pair_in, left.astype(jnp.bfloat16), right.astype(jnp.bfloat16))  3.24 us
    dot_general x1, matrix products, on_device(): jnp.einsum('kid,kjd->ijd', lax.all_gather(left_lines, 'pc', axis=1, tiled...  2.35 us
  transfers between devices with their start and end apart: 2, of which 2 were waited for; matrix products, arithmetic and copies ran while one was open for 4% of the time, Pallas kernels for 0%

commit v1 on v0

--- a/solution.py
+++ b/solution.py
@@ -2,6 +2,12 @@
 import jax.numpy as jnp
 from jax import lax
 from jax.sharding import PartitionSpec as P
+
+
+def swap_blocks(value, axis, split, join):
+    pieces = jnp.split(value, lax.axis_size(axis), axis=split)
+    received = lax.all_to_all(jnp.stack(pieces), axis, 0, 0)
+    return jnp.concatenate(received, axis=join)
 
 
 def unit_channels(values, channel_gain):
@@ -42,7 +48,7 @@
     ready, left, right = make_factors(pair_array, left_weight, right_weight, left_gate, right_gate)
     count = pair_array.shape[0] * lax.axis_size("pr")
     left_lines, right_lines = (
-        lax.all_to_all(left, "pr", split_axis=2, concat_axis=0, tiled=True),
+        swap_blocks(left, "pr", 2, 0),
         lax.all_to_all(right, "pr", split_axis=2, concat_axis=0, tiled=True),
     )
     strip = jnp.einsum(

time: 105 us -> 117 us (1.11)
  local copies, waits for them, and re-layouts: 13.5 us -> 25.5 us
    another operation x0 -> x10, local copies, waits for them, and re-layouts: none -> 7.74 us  [swap_blocks(): received = lax.all_to_all(jnp.stack(pieces), axis, 0, 0)]
    unnamed x18 -> x25, local copies, waits for them, and re-layouts: 6.59 us -> 12.8 us
    all_to_all x2 -> x0, local copies, waits for them, and re-layouts: 2.06 us -> none  [on_device(): lax.all_to_all(left, 'pr', split_axis=2, concat_axis=0, tiled=True)]
    reshape x0 -> x1, local copies, waits for them, and re-layouts: none -> 1.65 us  [swap_blocks(): return jnp.concatenate(received, axis=join)]
    convert_element_type x2 -> x1, local copies, waits for them, and re-layouts: 3.24 us -> 1.62 us  [make_factors(): return (pair_in, left.astype(jnp.bfloat16), right.astype(jnp.bfloat16))]
where the time goes in v1:
time: 117 us; the launch traced here: 116 us
  waiting for transfers between devices  38.2 us (33%)
  blocking collectives  26.8 us (23%)
  local copies, waits for them, and re-layouts  25.5 us (22%)
  between operations  13.6 us (12%)
  matrix products  6.95 us (6%)
  starting transfers between devices  3.84 us (3%)
  other arithmetic  1.27 us (1%)
    all_gather x1, waiting for transfers between devices, on_device(): lax.all_gather(left_lines, 'pc', axis=1, tiled=True)  28.9 us
    all_to_all x1, blocking collectives, swap_blocks(): received = lax.all_to_all(jnp.stack(pieces), axis, 0, 0)  14.7 us
    unnamed x25, local copies, waits for them, and re-layouts  12.8 us
    all_to_all x1, blocking collectives, on_device(): lax.all_to_all(right, 'pr', split_axis=2, concat_axis=0, tiled=True)  12.1 us
    all_to_all x1, waiting for transfers between devices, on_device(): mixed = lax.all_to_all(strip, 'pr', split_axis=0, concat_axis=2, tiled=True)  9.28 us
    another operation x10, local copies, waits for them, and re-layouts, swap_blocks(): received = lax.all_to_all(jnp.stack(pieces), axis, 0, 0)  7.74 us
    all_to_all x1, starting transfers between devices, on_device(): mixed = lax.all_to_all(strip, 'pr', split_axis=0, concat_axis=2, tiled=True)  3.83 us
    dot_general x1, matrix products, on_device(): jnp.einsum('kid,kjd->ijd', lax.all_gather(left_lines, 'pc', axis=1, tiled...  2.35 us
  transfers between devices with their start and end apart: 2, of which 2 were waited for; matrix products, arithmetic and copies ran while one was open for 4% of the time, Pallas kernels for 0%

profile of v1, /device:TPU:0, one launch (start us, length us, event | category | flops | bytes accessed | tf_op | source)
XLA Modules:
  0.0 116.2 jit_solution(363312956391407247)
XLA Ops:
  6.5 1.0 copy-done
  7.6 1.0 fusion.24
  8.6 1.2 %fusion.14 = bf16[32,64,128]{2,1,0:T(8,128)(2,1)S(1)} fusion(f32[32,64,128]{2,1,0:T(8,128)S(1)} %fusion.24, bf16[32,64,128]{2,1,0:T(8,128)(2,1)S(1)} %copy-done, bf16[128,128]{1,0:T(8,128)(2,1)} %param.11), kind=kOutput, calls=%fused_computation.22 | convolution fusion | flops 68419584 | bytes 2129920 | tf_op jit(solution)/shard_map/ijc,cd->ijd/dot_general | solution.py:25
  9.8 2.3 %slice_bitcast_fusion = (bf16[1,32,64,16]{3,2,1,0:T(8,128)(2,1)S(1)}, bf16[1,32,64,16]{3,2,1,0:T(8,128)(2,1)S(1)}, bf16[1,32,64,16]{3,2,1,0:T(8,128)(2,1)S(1)}, ...) fusion(bf16[32,64,128]{2,1,0:T(8,128)(2,1)S(1)} %fusion.14), kind=kLoop, calls=%fused_computation.29 | loop fusion | bytes 1048576 | tf_op jit(solution)/shard_map/stack | solution.py:9
  12.1 1.2 %copy.39 = bf16[1,32,64,16]{2,3,1,0:T(8,128)(2,1)S(1)} copy(bf16[1,32,64,16]{3,2,1,0:T(8,128)(2,1)} %get-tuple-element.12) | data formatting | bytes 131072 | tf_op jit(solution)/shard_map/stack | solution.py:9
  13.4 0.7 constant_dynamic-update-slice_fusion.7
  14.0 1.2 %copy.40 = bf16[1,32,64,16]{2,3,1,0:T(8,128)(2,1)S(1)} copy(bf16[1,32,64,16]{3,2,1,0:T(8,128)(2,1)} %get-tuple-element.11) | data formatting | bytes 131072 | tf_op jit(solution)/shard_map/stack | solution.py:9
  15.3 1.2 %copy.41 = bf16[1,32,64,16]{2,3,1,0:T(8,128)(2,1)S(1)} copy(bf16[1,32,64,16]{3,2,1,0:T(8,128)(2,1)} %get-tuple-element.10) | data formatting | bytes 131072 | tf_op jit(solution)/shard_map/stack | solution.py:9
  16.5 0.2 copy.42
  16.7 0.2 copy.43
  16.9 0.2 copy.44
  17.1 0.2 copy.45
  17.4 0.2 copy.46
  17.6 0.7 constant_dynamic-update-slice_fusion.6
  18.2 0.7 constant_dynamic-update-slice_fusion.5
  18.9 0.7 constant_dynamic-update-slice_fusion.4
  19.6 0.7 constant_dynamic-update-slice_fusion.3
  20.2 0.7 constant_dynamic-update-slice_fusion.2
  20.9 0.7 constant_dynamic-update-slice_fusion.1
  21.5 0.7 constant_dynamic-update-slice_fusion
  22.2 2.3 %reshape.32 = bf16[8,2,16384]{2,1,0:T(2,128)(2,1)S(1)} reshape(bf16[8,32,16,64]{3,2,1,0:T(8,128)(2,1)} %bitcast.79) | data formatting | bytes 1048576
  24.5 14.7 %all_to_all.32 = bf16[8,2,16384]{2,1,0:T(2,128)(2,1)S(1)} all-to-all(bf16[8,2,16384]{2,1,0:T(2,128)(2,1)S(1)} %reshape.32), channel_id=1, replica_groups=mesh['pr'=8,'pc'=4] {'pr'}, dimensions={0} | all-to-all | bytes 1048576 | tf_op jit(solution)/shard_map/all_to_all | solution.py:9
  39.2 0.7 reshape.33
  39.9 1.6 %copy.47 = bf16[256,64,16]{0,1,2:T(8,128)(2,1)} copy(bf16[256,64,16]{1,2,0:T(8,128)(2,1)S(1)} %bitcast.75) | data formatting | bytes 1048576 | tf_op jit(solution)/shard_map/reshape | solution.py:10
  41.5 0.0 all-gather.2.cloned.1.call-update
  41.6 0.3 fusion.27
  41.9 0.4 fusion.15
  42.3 1.6 %copy.36 = bf16[32,64,128]{1,0,2:T(8,128)(2,1)S(1)} copy(bf16[32,64,128]{2,1,0:T(8,128)(2,1)S(1)} %fusion.15) | data formatting | bytes 1048576 | tf_op jit(solution)/shard_map/convert_element_type | solution.py:31
  43.9 0.7 reshape.34
  44.6 12.1 %all_to_all.33 = bf16[8,2,16384]{2,1,0:T(2,128)(2,1)S(1)} all-to-all(bf16[8,2,16384]{2,1,0:T(2,128)(2,1)S(1)} %reshape.34), channel_id=1, replica_groups=mesh['pr'=8,'pc'=4] {'pr'}, dimensions={0} | all-to-all | bytes 1048576 | tf_op jit(solution)/shard_map/all_to_all | solution.py:52
  56.8 0.7 reshape.35
  57.4 0.4 copy.38
  57.8 28.9 %all-gather.2.cloned.1.call-done = bf16[256,256,16]{0,1,2:T(8,128)(2,1)} async-done(((bf16[256,64,16]{0,1,2:T(8,128)(2,1)}), bf16[256,256,16]{0,1,2:T(8,128)(2,1)}) %all-gather.2.cloned.1.call-update) | async-done | bytes 2097168 | tf_op jit(solution)/shard_map/all_gather | solution.py:56
  86.8 2.4 %fusion.18 = bf16[256,64,16]{0,1,2:T(8,128)(2,1)S(1)} fusion(bf16[256,256,16]{0,1,2:T(8,128)(2,1)} %all-gather.2.cloned.1.call-done, bf16[256,64,16]{1,2,0:T(8,128)(2,1)S(1)} %bitcast.74), kind=kOutput, calls=%fused_computation.26 | convolution fusion | flops 134742016 | bytes 3145728 | tf_op jit(solution)/shard_map/kid,kjd->ijd/dot_general | solution.py:54
  89.1 1.0 copy.49
  90.1 1.5 %reshape.36 = bf16[8,2,16384]{2,1,0:T(2,128)(2,1)} reshape(bf16[256,16,64]{2,1,0:T(8,128)(2,1)S(1)} %bitcast.77) | data formatting | bytes 1048576
  91.6 3.8 %all-to-all-start.2 = ((bf16[8,2,16384]{2,1,0:T(2,128)(2,1)}), bf16[8,2,16384]{2,1,0:T(2,128)(2,1)S(1)}, u32[]{:S(2)}, u32[]{:S(2)}) async-start(bf16[8,2,16384]{2,1,0:T(2,128)(2,1)} %reshape.36), calls=%async_computation.2 | async-start | bytes 1048576 | tf_op jit(solution)/shard_map/all_to_all | solution.py:61
  95.4 0.4 fusion.13
  95.9 9.3 %all-to-all-done.2 = bf16[8,2,16384]{2,1,0:T(2,128)(2,1)S(1)} async-done(((bf16[8,2,16384]{2,1,0:T(2,128)(2,1)}), bf16[8,2,16384]{2,1,0:T(2,128)(2,1)S(1)}, u32[]{:S(2)}, u32[]{:S(2)}) %all-to-all-start.2) | async-done | bytes 524320 | tf_op jit(solution)/shard_map/all_to_all | solution.py:61
  105.1 0.7 reshape.37
  105.8 0.2 convert_bitcast_fusion
  106.0 0.2 fusion.19
  106.2 0.4 multiply_reduce_fusion
  106.7 0.3 copy.50
  106.9 0.4 copy-done.3
  107.3 0.5 fusion.2
  107.8 0.3 copy-done.2
  108.1 1.3 %fusion.17 = bf16[32,64,128]{2,1,0:T(8,128)(2,1)} fusion(f32[32,64,128]{2,1,0:T(8,128)S(1)} %fusion.13, bf16[32,64,128]{1,2,0:T(8,128)(2,1)S(1)} %fusion.2, bf16[128,128]{1,0:T(8,128)(2,1)S(1)} %copy-done.2), kind=kOutput, calls=%fused_computation.25 | convolution fusion | flops 67633152 | bytes 2129920 | tf_op jit(solution)/shard_map/ijd,dc->ijc/dot_general | solution.py:41
  (12 shorter events, 0.0 us)
Async XLA Ops:
  6.5 1.0 copy-start
  6.5 80.2 %all-gather.2.cloned.1.call-start = ((), (), s32[]{:S(2)}) async-start(), calls=%async_computation.3 | async-start | bytes 2621440 | tf_op jit(solution)/shard_map/all_gather | solution.py:56
  39.2 2.3 %copy-start.1 = (bf16[128,128]{1,0:T(8,128)(2,1)S(1)}, bf16[128,128]{1,0:T(8,128)(2,1)}, u32[]{:S(2)}) copy-start(bf16[128,128]{1,0:T(8,128)(2,1)} %param.10) | copy-start | bytes 98308
  39.9 2.0 %copy-start.4 = (bf16[128,128]{1,0:T(8,128)(2,1)S(1)}, bf16[128,128]{1,0:T(8,128)(2,1)}, u32[]{:S(2)}) copy-start(bf16[128,128]{1,0:T(8,128)(2,1)} %param.12) | copy-start | bytes 98308
  89.1 6.3 %copy-start.5 = (bf16[128,128]{1,0:T(8,128)(2,1)S(1)}, bf16[128,128]{1,0:T(8,128)(2,1)}, u32[]{:S(2)}) copy-start(bf16[128,128]{1,0:T(8,128)(2,1)} %param.15) | copy-start | bytes 98308
  91.6 13.5 %all-to-all-start.2 = ((bf16[8,2,16384]{2,1,0:T(2,128)(2,1)}), bf16[8,2,16384]{2,1,0:T(2,128)(2,1)S(1)}, u32[]{:S(2)}, u32[]{:S(2)}) async-start(bf16[8,2,16384]{2,1,0:T(2,128)(2,1)} %reshape.36), calls=%async_computation.2 | async-start | bytes 1048576 | tf_op jit(solution)/shard_map/all_to_all | solution.py:61
  106.6 0.7 copy-start.3
  107.3 0.8 copy-start.2
Sparse Core Ops, SparseCore 0:
  41.7 45.0 all-gather.1
